TPU v7x, 32 devices: a whole 2x2x4 slice. The times are simulated.
32 devices in a mesh: leaf: 2 (over core), row: 4 (over y, x), col: 4 (over z).
Axes of the slice: x: 2, y: 2, z: 4, core: 2. Of those that a mesh axis runs over, the one named last changes fastest.
Arguments:
- rhs_leaf: bfloat16 [2, 8, 64, 2048], P('leaf', None, None, 'col'), may hold values from -6 to 6
- dinv_leaf: bfloat16 [2, 8, 2048, 2048], P('leaf', None, 'row', 'col'), as said below
- panel_leaf: bfloat16 [2, 8, 1024, 2048], P('leaf', None, 'col', 'row'), may hold values from -0.0625 to 0.0625
- counts: int32 [2, 8], P('leaf'), may hold values from 256 to 2048, as said below
- row_index: int32 [2, 8, 1024], P('leaf'), may hold values from 0 to 4095, as said below
- rhs_root: bfloat16 [64, 4096], P(None, 'col'), may hold values from -6 to 6
- dinv_root: bfloat16 [4096, 4096], P(('leaf', 'row')), as said below
Outputs:
- y_leaf: bfloat16 [2, 8, 64, 2048], P('leaf', None, None, 'row')
- y_root: bfloat16 [64, 4096], P(None, ('leaf', 'row'))
Inputs may be any that keep to these rules, and one draw needn't show every extreme that they name: `counts`: each subtree supernode has at least 256 columns; at least one supernode of every draw has all 2048. `row_index`: within one supernode the 1024 entries are distinct and increasing. `dinv_leaf`: each [2048, 2048] block is lower triangular with a nonzero diagonal. `dinv_root`: lower triangular with a nonzero diagonal.
All inputs are finite; a program needn't handle non-finite values.
Results may differ from a plain program's by a relative error of at most 0.0053.
Values may be sent and summed in bfloat16 or wider, within the bound.
No kernel may reach another device: no remote copies, remote signals or barrier semaphores. Data moves between devices by JAX's collectives and lax.ppermute only.
A program may use at most 64 MiB of HBM per device.

v0:
```python
import jax
import jax.numpy as jnp
from jax import lax
from jax.sharding import PartitionSpec as P


def local(rhs_leaf, dinv_leaf, panel_leaf, counts, row_index, rhs_root, dinv_root):
    width_col = rhs_leaf.shape[3]
    width_row = dinv_leaf.shape[2]
    panel_rows = panel_leaf.shape[2]
    columns = rhs_root.shape[0]
    sep_width = rhs_root.shape[1] * lax.axis_size("col")
    limit = counts[0][:, None, None]
    col_slots = lax.axis_index("col") * width_col + lax.iota(jnp.int32, width_col)
    masked = jnp.where(col_slots[None, None, :] < limit, rhs_leaf[0], jnp.zeros((), jnp.bfloat16))
    partial_value = jnp.einsum(
        "kbj,kij->kbi", masked, dinv_leaf[0], preferred_element_type=jnp.float32
    )
    summed = lax.psum(partial_value, "col")
    row_slots = lax.axis_index("row") * width_row + lax.iota(jnp.int32, width_row)
    live_rows = (row_slots[None, None, :] < limit).astype(jnp.float32)
    solved = (summed * live_rows).astype(jnp.bfloat16)
    update = jnp.einsum("kbi,kri->kbr", solved, panel_leaf[0], preferred_element_type=jnp.float32)
    offset = lax.axis_index("col") * panel_rows
    targets = lax.dynamic_slice_in_dim(row_index[0], offset, panel_rows, 1)
    flat_update = jnp.transpose(update, (1, 0, 2)).reshape(columns, -1)
    accum = jnp.zeros((columns, sep_width), jnp.float32).at[:, targets.reshape(-1)].add(flat_update)
    piece = lax.psum_scatter(accum, "col", scatter_dimension=1, tiled=True)
    share = lax.psum(piece, ("leaf", "row"))
    reduced = (rhs_root.astype(jnp.float32) - share).astype(jnp.bfloat16)
    whole_reduced = lax.all_gather(reduced, "col", axis=1, tiled=True)
    y_root = jnp.dot(whole_reduced, dinv_root.T, preferred_element_type=jnp.float32).astype(
        jnp.bfloat16
    )
    return (solved[None], y_root)


def solution(mesh):
    in_specs = (
        P("leaf", None, None, "col"),
        P("leaf", None, "row", "col"),
        P("leaf", None, "col", "row"),
        P("leaf", None),
        P("leaf", None, None),
        P(None, "col"),
        P(("leaf", "row"), None),
    )
    out_specs = (P("leaf", None, None, "row"), P(None, ("leaf", "row")))
    return jax.shard_map(local, mesh=mesh, in_specs=in_specs, out_specs=out_specs, check_vma=False)
```

profile of v0, /device:TPU:0, one launch (start us, length us, event | category | flops | bytes accessed | tf_op | source)
XLA Modules:
  0.0 218.8 jit_solution(5079778243573968000)
XLA Ops:
  7.2 0.0 copy-start
  7.2 0.0 all-reduce.3.cloned.1.call-start
  7.2 0.9 compare_convert_fusion
  8.1 4.7 %fusion = f32[8,64,512]{2,1,0:T(8,128)} fusion(bf16[1,8,512,512]{3,2,1,0:T(8,128)(2,1)} %param.8, bf16[1,8,64,512]{3,2,1,0:T(8,128)(2,1)} %param.7, pred[8,512]{1,0:T(8,128)(4,1)S(1)} %get-tuple-element.3), kind=kOutput, calls=%fused_computation.1 | convolution fusion | flops 268697600 | bytes 5771264 | tf_op jit(solution)/shard_map/kbj,kij->kbi/dot_general | solution.py:16
  12.8 0.0 all-reduce.3.cloned.1.call-update
  12.8 0.0 reduce-scatter.2.cloned.1.call-start
  12.9 0.7 dynamic-slice_bitcast_fusion
  13.6 54.0 %all-reduce.3.cloned.1.call-done = f32[8,64,512]{2,1,0:T(8,128)} async-done(((f32[8,64,512]{2,1,0:T(8,128)}), f32[8,64,512]{2,1,0:T(8,128)}) %all-reduce.3.cloned.1.call-update) | async-done | bytes 1048592 | tf_op jit(solution)/shard_map/psum | solution.py:19
  67.6 0.0 copy-done
  67.6 2.0 fusion.4
  69.6 0.1 copy.13
  69.7 1.3 copy.12
  71.0 13.3 %scatter_custom_fusion = f32[64,4096]{0,1:T(8,128)} fusion(s32[2048]{0:T(1024)S(1)} %bitcast.29, f32[2048,64]{1,0:T(8,128)} %copy.12, f32[]{:T(128)} %constant.7.clone.1), kind=kCustom, calls=%fused_computation.7 | custom fusion | flops 131072 | bytes 1049088 | tf_op jit(solution)/shard_map/scatter-add | solution.py:27
  84.3 0.0 reduce-scatter.2.cloned.1.call-update
  84.3 0.0 all-reduce.5.cloned.1.call-start
  84.4 0.0 copy-done.2
  84.4 0.2 copy.10
  84.6 42.8 %reduce-scatter.2.cloned.1.call-done = f32[64,1024]{0,1:T(8,128)} async-done(((f32[64,4096]{0,1:T(8,128)}), f32[64,1024]{0,1:T(8,128)}) %reduce-scatter.2.cloned.1.call-update) | async-done | bytes 262160 | tf_op jit(solution)/shard_map/reduce_scatter | solution.py:28
  127.4 0.0 all-reduce.5.cloned.1.call-update
  127.4 0.9 fusion.11
  128.4 56.2 %all-reduce.5.cloned.1.call-done = f32[64,1024]{0,1:T(8,128)} async-done(((f32[64,1024]{0,1:T(8,128)}), f32[64,1024]{0,1:T(8,128)}) %all-reduce.5.cloned.1.call-update) | async-done | bytes 262160 | tf_op jit(solution)/shard_map/psum | solution.py:29
  184.5 1.1 subtract_convert_fusion
  185.6 22.4 %all_gather.3 = bf16[64,4096]{0,1:T(8,128)(2,1)S(1)} all-gather(bf16[64,1024]{0,1:T(8,128)(2,1)S(1)} %subtract_convert_fusion), channel_id=1, replica_groups=mesh['leaf'=2,'row'=4,'col'=4] {'col'}, dimensions={1}, use_global_device_ids=true | all-gather | bytes 655360 | tf_op jit(solution)/shard_map/all_gather | solution.py:31
  208.0 4.2 %convolution_convert_fusion = bf16[64,512]{1,0:T(8,128)(2,1)} fusion(bf16[64,4096]{0,1:T(8,128)(2,1)S(1)} %all_gather.3, bf16[512,4096]{1,0:T(8,128)(2,1)} %param.13), kind=kOutput, calls=%fused_computation.6 | convolution fusion | flops 268468224 | bytes 4784128 | tf_op jit(solution)/shard_map/dot_general | solution.py:32
  (6 shorter events, 0.0 us)
Async XLA Ops:
  7.2 60.5 %copy-start = (bf16[1,8,256,512]{3,2,1,0:T(8,128)(2,1)S(1)}, bf16[1,8,256,512]{3,2,1,0:T(8,128)(2,1)}, u32[]{:S(2)}) copy-start(bf16[1,8,256,512]{3,2,1,0:T(8,128)(2,1)} %param.9) | copy-start | bytes 6291460
  7.2 60.4 %all-reduce.3.cloned.1.call-start = ((), (), s32[]{:S(2)}) async-start(), calls=%async_computation.1 | async-start | bytes 2097152 | tf_op jit(solution)/shard_map/psum | solution.py:19
  12.8 114.6 %reduce-scatter.2.cloned.1.call-start = ((), (), s32[]{:S(2)}) async-start(), calls=%async_computation.2 | async-start | bytes 2621440 | tf_op jit(solution)/shard_map/reduce_scatter | solution.py:28
  71.0 13.4 %copy-start.2 = (bf16[64,1024]{1,0:T(8,128)(2,1)S(1)}, bf16[64,1024]{1,0:T(8,128)(2,1)}, u32[]{:S(2)}) copy-start(bf16[64,1024]{1,0:T(8,128)(2,1)} %param.12) | copy-start | bytes 393220
  71.0 56.5 %copy-start.1 = (f32[8,64,512]{2,1,0:T(8,128)S(1)}, f32[8,64,512]{2,1,0:T(8,128)}, u32[]{:S(2)}) copy-start(f32[8,64,512]{2,1,0:T(8,128)} %all-reduce.3.cloned.1.call-done) | copy-start | bytes 3145732
  84.3 100.2 %all-reduce.5.cloned.1.call-start = ((), (), s32[]{:S(2)}) async-start(), calls=%async_computation.3 | async-start | bytes 1048576 | tf_op jit(solution)/shard_map/psum | solution.py:29
Sparse Core Ops, SparseCore 0:
  13.0 54.6 all-reduce.2
  84.5 42.8 reduce-scatter.1
  130.5 53.9 all-reduce.4
where the time goes:
time: 219 us
  waiting for transfers between devices  153 us (70%)
  blocking collectives  22.4 us (10%)
  other arithmetic  16.2 us (7%)
  between operations  13.8 us (6%)
  matrix products  10.9 us (5%)
  local copies, waits for them, and re-layouts  2.27 us (1%)
    psum x1, waiting for transfers between devices, local(): share = lax.psum(piece, ('leaf', 'row'))  56.2 us
    psum x1, waiting for transfers between devices, local(): summed = lax.psum(partial_value, 'col')  54 us
    reduce_scatter x1, waiting for transfers between devices, local(): piece = lax.psum_scatter(accum, 'col', scatter_dimension=1, tiled=True)  42.8 us
    all_gather x1, blocking collectives, local(): whole_reduced = lax.all_gather(reduced, 'col', axis=1, tiled=True)  22.4 us
    scatter-add x1, other arithmetic, local(): jnp.zeros((columns, sep_width), jnp.float32).at[:, targets.reshape(-1)]  13.3 us
    dot_general x1, matrix products, local(): jnp.einsum('kbj,kij->kbi', masked, dinv_leaf[0], preferred_element_type=j...  4.71 us
  transfers between devices with their start and end apart: 3, of which 3 were waited for; matrix products, arithmetic and copies ran while one was open for 1% of the time, Pallas kernels for 0%

commit v1 on v0

--- a/solution.py
+++ b/solution.py
@@ -26,7 +26,7 @@
     flat_update = jnp.transpose(update, (1, 0, 2)).reshape(columns, -1)
     accum = jnp.zeros((columns, sep_width), jnp.float32).at[:, targets.reshape(-1)].add(flat_update)
     piece = lax.psum_scatter(accum, "col", scatter_dimension=1, tiled=True)
-    share = lax.psum(piece, ("leaf", "row"))
+    share = lax.psum(lax.psum(piece, "row"), "leaf")
     reduced = (rhs_root.astype(jnp.float32) - share).astype(jnp.bfloat16)
     whole_reduced = lax.all_gather(reduced, "col", axis=1, tiled=True)
     y_root = jnp.dot(whole_reduced, dinv_root.T, preferred_element_type=jnp.float32).astype(

time: 219 us -> 231 us (1.055)
  waiting for transfers between devices: 153 us -> 164 us
    psum x1 -> x2, waiting for transfers between devices: 56.2 us -> 67.2 us  [local(): share = lax.psum(lax.psum(piece, 'row'), 'leaf')]
  transfers between devices with their start and end apart: 3 -> 4, of which waited for: 3 -> 4; matrix products, arithmetic and copies ran while one was open for 1% -> 1% of each run, Pallas kernels for 0% -> 0%
where the time goes in v1:
time: 231 us; the launch traced here: 230 us
  waiting for transfers between devices  164 us (71%)
  blocking collectives  22.9 us (10%)
  other arithmetic  16.1 us (7%)
  between operations  13.8 us (6%)
  matrix products  10.9 us (5%)
    psum x2, waiting for transfers between devices, local(): share = lax.psum(lax.psum(piece, 'row'), 'leaf')  67.2 us
    psum x1, waiting for transfers between devices, local(): summed = lax.psum(partial_value, 'col')  54 us
    reduce_scatter x1, waiting for transfers between devices, local(): piece = lax.psum_scatter(accum, 'col', scatter_dimension=1, tiled=True)  43 us
    all_gather x1, blocking collectives, local(): whole_reduced = lax.all_gather(reduced, 'col', axis=1, tiled=True)  22.9 us
    scatter-add x1, other arithmetic, local(): jnp.zeros((columns, sep_width), jnp.float32).at[:, targets.reshape(-1)]  13.2 us
    dot_general x1, matrix products, local(): jnp.einsum('kbj,kij->kbi', masked, dinv_leaf[0], preferred_element_type=j...  4.71 us
  transfers between devices with their start and end apart: 4, of which 4 were waited for; matrix products, arithmetic and copies ran while one was open for 1% of the time, Pallas kernels for 0%

profile of v1, /device:TPU:0, one launch (start us, length us, event | category | flops | bytes accessed | tf_op | source)
XLA Modules:
  0.0 230.4 jit_solution(4059251930167812860)
XLA Ops:
  7.2 0.0 all-reduce.4.cloned.1.call-start
  7.2 0.9 compare_convert_fusion
  8.1 4.7 %fusion = f32[8,64,512]{2,1,0:T(8,128)} fusion(bf16[1,8,512,512]{3,2,1,0:T(8,128)(2,1)} %param.8, bf16[1,8,64,512]{3,2,1,0:T(8,128)(2,1)} %param.7, pred[8,512]{1,0:T(8,128)(4,1)S(1)} %get-tuple-element.3), kind=kOutput, calls=%fused_computation.1 | convolution fusion | flops 268697600 | bytes 5771264 | tf_op jit(solution)/shard_map/kbj,kij->kbi/dot_general | solution.py:16
  12.8 0.0 all-reduce.4.cloned.1.call-update
  12.8 0.0 reduce-scatter.2.cloned.1.call-start
  12.9 0.7 dynamic-slice_bitcast_fusion
  13.6 54.0 %all-reduce.4.cloned.1.call-done = f32[8,64,512]{2,1,0:T(8,128)} async-done(((f32[8,64,512]{2,1,0:T(8,128)}), f32[8,64,512]{2,1,0:T(8,128)}) %all-reduce.4.cloned.1.call-update) | async-done | bytes 1048592 | tf_op jit(solution)/shard_map/psum | solution.py:19
  67.6 2.0 fusion.4
  69.6 0.1 copy.13
  69.7 1.3 copy.12
  71.0 13.2 %scatter_custom_fusion = f32[64,4096]{0,1:T(8,128)} fusion(s32[2048]{0:T(1024)S(1)} %bitcast.29, f32[2048,64]{1,0:T(8,128)} %copy.12, f32[]{:T(128)} %constant.7.clone.1), kind=kCustom, calls=%fused_computation.7 | custom fusion | flops 131072 | bytes 1049088 | tf_op jit(solution)/shard_map/scatter-add | solution.py:27
  84.2 0.0 reduce-scatter.2.cloned.1.call-update
  84.2 0.0 all-reduce.6.cloned.1.call-start
  84.3 43.0 %reduce-scatter.2.cloned.1.call-done = f32[64,1024]{0,1:T(8,128)} async-done(((f32[64,4096]{0,1:T(8,128)}), f32[64,1024]{0,1:T(8,128)}) %reduce-scatter.2.cloned.1.call-update) | async-done | bytes 262160 | tf_op jit(solution)/shard_map/reduce_scatter | solution.py:28
  127.3 0.0 all-reduce.6.cloned.1.call-update
  127.3 0.0 all-reduce.8.cloned.1.call-start
  127.4 0.2 copy.10
  127.6 47.3 %all-reduce.6.cloned.1.call-done = f32[64,1024]{0,1:T(8,128)} async-done(((f32[64,1024]{0,1:T(8,128)}), f32[64,1024]{0,1:T(8,128)}) %all-reduce.6.cloned.1.call-update) | async-done | bytes 262160 | tf_op jit(solution)/shard_map/psum | solution.py:29
  174.9 0.0 all-reduce.8.cloned.1.call-update
  174.9 0.9 fusion.11
  175.8 19.9 %all-reduce.8.cloned.1.call-done = f32[64,1024]{0,1:T(8,128)} async-done(((f32[64,1024]{0,1:T(8,128)}), f32[64,1024]{0,1:T(8,128)}) %all-reduce.8.cloned.1.call-update) | async-done | bytes 262160 | tf_op jit(solution)/shard_map/psum | solution.py:29
  195.7 1.1 subtract_convert_fusion
  196.8 22.9 %all_gather.3 = bf16[64,4096]{0,1:T(8,128)(2,1)S(1)} all-gather(bf16[64,1024]{0,1:T(8,128)(2,1)S(1)} %subtract_convert_fusion), channel_id=1, replica_groups=mesh['leaf'=2,'row'=4,'col'=4] {'col'}, dimensions={1}, use_global_device_ids=true | all-gather | bytes 655360 | tf_op jit(solution)/shard_map/all_gather | solution.py:31
  219.7 4.2 %convolution_convert_fusion = bf16[64,512]{1,0:T(8,128)(2,1)} fusion(bf16[64,4096]{0,1:T(8,128)(2,1)S(1)} %all_gather.3, bf16[512,4096]{1,0:T(8,128)(2,1)} %param.13), kind=kOutput, calls=%fused_computation.6 | convolution fusion | flops 268468224 | bytes 4784128 | tf_op jit(solution)/shard_map/dot_general | solution.py:32
  (9 shorter events, 0.0 us)
Async XLA Ops:
  7.2 60.5 %copy-start = (bf16[1,8,256,512]{3,2,1,0:T(8,128)(2,1)S(1)}, bf16[1,8,256,512]{3,2,1,0:T(8,128)(2,1)}, u32[]{:S(2)}) copy-start(bf16[1,8,256,512]{3,2,1,0:T(8,128)(2,1)} %param.9) | copy-start | bytes 6291460
  7.2 60.4 %all-reduce.4.cloned.1.call-start = ((), (), s32[]{:S(2)}) async-start(), calls=%async_computation.1 | async-start | bytes 2097152 | tf_op jit(solution)/shard_map/psum | solution.py:19
  12.8 114.5 %reduce-scatter.2.cloned.1.call-start = ((), (), s32[]{:S(2)}) async-start(), calls=%async_computation.2 | async-start | bytes 2621440 | tf_op jit(solution)/shard_map/reduce_scatter | solution.py:28
  71.0 56.4 %copy-start.2 = (bf16[64,1024]{1,0:T(8,128)(2,1)S(1)}, bf16[64,1024]{1,0:T(8,128)(2,1)}, u32[]{:S(2)}) copy-start(bf16[64,1024]{1,0:T(8,128)(2,1)} %param.12) | copy-start | bytes 393220
  84.2 90.7 %copy-start.1 = (f32[8,64,512]{2,1,0:T(8,128)S(1)}, f32[8,64,512]{2,1,0:T(8,128)}, u32[]{:S(2)}) copy-start(f32[8,64,512]{2,1,0:T(8,128)} %all-reduce.4.cloned.1.call-done) | copy-start | bytes 3145732
  84.2 90.6 %all-reduce.6.cloned.1.call-start = ((), (), s32[]{:S(2)}) async-start(), calls=%async_computation.3 | async-start | bytes 1048576 | tf_op jit(solution)/shard_map/psum | solution.py:29
  127.3 68.4 %all-reduce.8.cloned.1.call-start = ((), (), s32[]{:S(2)}) async-start(), calls=%async_computation.4 | async-start | bytes 1048576 | tf_op jit(solution)/shard_map/psum | solution.py:29
Sparse Core Ops, SparseCore 0:
  13.0 54.6 all-reduce.3
  84.4 42.8 reduce-scatter.1
  130.3 44.5 all-reduce.5
  177.1 18.5 all-reduce.7
